TPU v7x, 512 devices: a whole 4x8x8 slice. The times are simulated.
512 devices in a mesh: owner: 64 (over y, x, core), rows: 8 (over z).
Axes of the slice: x: 4, y: 8, z: 8, core: 2. Of those that a mesh axis runs over, the one named last changes fastest.
Arguments:
- train_down: float32 [64, 1024, 2048], P('owner', None, 'rows'), may hold values from -0.1875 to 0.1875
- router_weight: float32 [2048, 64], P('rows', 'owner'), may hold values from -0.125 to 0.125
- router_gain: float32 [2048], P('rows'), may hold values from 0.25 to 1.75
Outputs:
- ready_down: bfloat16 [64, 2048, 1024], P('owner')
- serve_router: bfloat16 [2048, 64], replicated
All inputs are finite; a program needn't handle non-finite values.
Results may differ from a plain program's by a relative error of at most 0.001.
Values may be sent and summed in bfloat16 or wider, within the bound.
A program may use at most 64 MiB of HBM per device.

v0:
```python
import jax
import jax.numpy as jnp
from jax import lax
from jax.sharding import PartitionSpec as P


def in_order(blocks, dim):
    blocks = jnp.moveaxis(blocks, 0, dim)
    dims = blocks.shape
    return blocks.reshape(*dims[:dim], dims[dim] * dims[dim + 1], *dims[dim + 2 :])


def from_everyone(array, axis):
    copies = jnp.broadcast_to(array, (lax.axis_size(axis), *array.shape))
    return lax.all_to_all(copies, axis, split_axis=0, concat_axis=0, tiled=True)


def gather_directly(array, axis, dim):
    return in_order(from_everyone(array, axis), dim)


def on_device(train_down, router_weight, router_gain):
    narrow_down = train_down.astype(jnp.bfloat16)
    ready_down = lax.all_gather(narrow_down, "rows", axis=2, tiled=True)
    ready_down = jnp.transpose(ready_down, (0, 2, 1))
    part_router = (router_weight * router_gain[:, None]).astype(jnp.bfloat16)
    row_router = lax.all_gather(part_router, "rows", axis=0, tiled=True)
    serve_router = gather_directly(row_router, "owner", 1)
    return (ready_down, serve_router)


def solution(mesh):
    in_specs = (P("owner", None, "rows"), P("rows", "owner"), P("rows"))
    out_specs = (P("owner", None, None), P())
    return jax.shard_map(
        on_device, mesh=mesh, in_specs=in_specs, out_specs=out_specs, check_vma=False
    )
```

profile of v0, /device:TPU:1, one launch (start us, length us, event | category | flops | bytes accessed | tf_op | source)
XLA Modules:
  0.0 85.6 jit_solution(9226915147789131716)
XLA Ops:
  7.2 0.0 all-gather.2.cloned.1.call-start
  7.2 2.2 %copy.7 = bf16[1,1024,256]{1,2,0:T(8,128)(2,1)} copy(f32[1,1024,256]{2,1,0:T(8,128)} %param.3) | data formatting | bytes 1572864 | tf_op args[0]
  9.4 0.0 all-gather.2.cloned.1.call-update
  9.5 0.7 multiply_convert_fusion
  10.2 19.4 %all_gather.9 = bf16[2048,1]{0,1:T(2,128)(2,1)S(1)} all-gather(bf16[256,1]{0,1:T(2,128)(2,1)S(1)} %multiply_convert_fusion), channel_id=1, replica_groups=mesh['owner'=64,'rows'=8] {'rows'}, dimensions={0}, use_global_device_ids=true | all-gather | bytes 4608 | tf_op jit(solution)/shard_map/all_gather | solution.py:27
  29.6 0.3 broadcast_bitcast_fusion
  29.9 0.5 broadcast.2
  30.4 2.2 %reduce.1 = bf16[64,2048]{1,0:T(8,128)(2,1)S(1)} reduce(bf16[64,1,2048]{2,1,0:T(2,128)(2,1)S(1)} %broadcast_bitcast_fusion, bf16[]{:T(256)} %broadcast.2), dimensions={1}, to_apply=%broadcast_bitcast_fusion.reduce_sub_computation | reduce | bytes 524290
  32.5 0.2 reshape.10
  32.7 27.4 %all_to_all.5 = bf16[64,2,1024]{2,1,0:T(2,128)(2,1)S(1)} all-to-all(bf16[64,2,1024]{2,1,0:T(2,128)(2,1)S(1)} %reshape.10), channel_id=1, replica_groups=mesh['owner'=64,'rows'=8] {'owner'}, dimensions={0} | all-to-all | bytes 524288 | tf_op jit(solution)/shard_map/all_to_all | solution.py:15
  60.2 0.2 reshape.11
  60.4 0.9 copy.10
  61.2 12.9 %all-gather.2.cloned.1.call-done = bf16[1,1024,2048]{1,2,0:T(8,128)(2,1)} async-done(((bf16[1,1024,256]{1,2,0:T(8,128)(2,1)}), bf16[1,1024,2048]{1,2,0:T(8,128)(2,1)}) %all-gather.2.cloned.1.call-update) | async-done | bytes 4194320 | tf_op jit(solution)/shard_map/all_gather | solution.py:24
  74.2 4.6 %copy.12 = bf16[1,2048,1024]{2,1,0:T(8,128)(2,1)} copy(bf16[1,2048,1024]{2,1,0:T(8,128)(2,1)} %bitcast.10) | data formatting | bytes 8388608
  (1 shorter events, 0.0 us)
Async XLA Ops:
  7.2 67.0 %all-gather.2.cloned.1.call-start = ((), (), s32[]{:S(2)}) async-start(), calls=%async_computation.1 | async-start | bytes 4718592 | tf_op jit(solution)/shard_map/all_gather | solution.py:24
Sparse Core Ops, SparseCore 0:
  10.6 63.4 all-gather.1
where the time goes:
time: 85.9 us; the launch traced here: 85.6 us
  blocking collectives  46.8 us (54%)
  between operations  14.1 us (16%)
  waiting for transfers between devices  12.9 us (15%)
  local copies, waits for them, and re-layouts  8.91 us (10%)
  other arithmetic  2.89 us (3%)
    all_to_all x1, blocking collectives, from_everyone(): return lax.all_to_all(copies, axis, split_axis=0, concat_axis=0, tiled=True)  27.4 us
    all_gather x1, blocking collectives, on_device(): row_router = lax.all_gather(part_router, 'rows', axis=0, tiled=True)  19.4 us
    all_gather x1, waiting for transfers between devices, on_device(): ready_down = lax.all_gather(narrow_down, 'rows', axis=2, tiled=True)  12.9 us
    unnamed x6, local copies, waits for them, and re-layouts  8.05 us
    unnamed x1, other arithmetic  2.15 us
  transfers between devices with their start and end apart: 1, of which 1 were waited for; matrix products, arithmetic and copies ran while one was open for 6% of the time, Pallas kernels for 0%

commit v1 on v0

v1 whole, which is shorter than its diff:
```python
import functools

import jax
import jax.numpy as jnp
from jax import lax
from jax.experimental import pallas as pl
from jax.experimental.pallas import tpu as pltpu
from jax.sharding import PartitionSpec as P

MESH = pl.DeviceIdType.MESH
NY, NX, NC, NZ = 8, 4, 2, 8
EXPERT = 1024
CUT = 256
LANES = 128
CHUNKS = EXPERT // LANES
HALF = CHUNKS // 2
FULL_STEPS = NZ // 2 - 1
EVENTS = FULL_STEPS * CHUNKS + HALF


def gather_kernel(
    down_ref, weight_ref, gain_ref,
    blocks_ref, router_ref,
    down, weight, gain, columns,
    in_sem, small_sem,
    send_up, recv_up, send_dn, recv_dn,
    send_z, recv_z, send_y, recv_y, send_x, recv_x, send_c, recv_c,
):
    owner = lax.axis_index("owner")
    z = lax.axis_index("rows")
    c = lax.rem(owner, NC)
    x = lax.rem(owner // NC, NX)
    y = owner // (NC * NX)

    def device(yy, xx, cc, zz):
        return {"owner": (yy * NX + xx) * NC + cc, "rows": zz}

    def z_peer(d):
        return device(y, x, c, lax.rem(z + d, NZ))

    def y_peer(d):
        return device(lax.rem(y + d, NY), x, c, z)

    def x_peer(d):
        return device(y, lax.rem(x + d, NX), c, z)

    def c_peer():
        return device(y, x, NC - 1 - c, z)

    loads = []
    for k in range(CHUNKS):
        part = pl.ds(k * LANES, LANES)
        loads.append(pltpu.make_async_copy(down_ref.at[part], down.at[part], in_sem.at[k]))
    load_weight = pltpu.make_async_copy(weight_ref, weight, small_sem.at[0])
    load_gain = pltpu.make_async_copy(gain_ref, gain, small_sem.at[1])
    loads[0].start()
    load_weight.start()
    load_gain.start()
    for k in range(1, CHUNKS):
        loads[k].start()

    barrier = pltpu.get_barrier_semaphore()
    peers = [z_peer(d) for d in range(1, NZ)] + [y_peer(d) for d in range(1, NY)]
    peers += [x_peer(d) for d in range(1, NX)] + [c_peer()]
    for peer in peers:
        pl.semaphore_signal(barrier, inc=1, device_id=peer, device_id_type=MESH)

    def turn(k):
        loads[k].wait()
        piece = down[k * LANES : (k + 1) * LANES, :]
        blocks_ref[z, k] = jnp.transpose(piece).astype(jnp.bfloat16)

    def remote(ref, send, recv, peer):
        return pltpu.make_async_remote_copy(
            src_ref=ref, dst_ref=ref, send_sem=send, recv_sem=recv,
            device_id=peer, device_id_type=MESH,
        )

    def chunk_up(step, k):
        slot = blocks_ref.at[lax.rem(z + NZ - step, NZ), k]
        i = step * CHUNKS + k
        return remote(slot, send_up.at[i], recv_up.at[i], z_peer(1))

    def chunk_dn(step, k):
        slot = blocks_ref.at[lax.rem(z + step, NZ), k]
        i = step * CHUNKS + (k if step < FULL_STEPS else k - HALF)
        return remote(slot, send_dn.at[i], recv_dn.at[i], z_peer(NZ - 1))

    def arrive_up(step, k):
        slot = blocks_ref.at[lax.rem(z + NZ - step - 1, NZ), k]
        i = step * CHUNKS + k
        remote(slot, send_up.at[i], recv_up.at[i], z_peer(1)).wait_recv()

    def arrive_dn(step, k):
        slot = blocks_ref.at[lax.rem(z + step + 1, NZ), k]
        i = step * CHUNKS + (k if step < FULL_STEPS else k - HALF)
        remote(slot, send_dn.at[i], recv_dn.at[i], z_peer(NZ - 1)).wait_recv()

    sent = []

    def send(copy):
        copy.start()
        sent.append(copy)

    turn(0)
    load_weight.wait()
    load_gain.wait()
    columns[y, x, c, z] = weight[...] * gain[...]
    turn(1)
    pl.semaphore_wait(barrier, len(peers))

    for d in range(1, NZ):
        send(remote(columns.at[y, x, c, z], send_z.at[d - 1], recv_z.at[d - 1], z_peer(d)))
    for k in range(CHUNKS):
        if k >= 1 and k + 1 < CHUNKS:
            turn(k + 1)
        send(chunk_up(0, k))
        send(chunk_dn(0, k))

    def router_y():
        for d in range(1, NZ):
            slot = columns.at[y, x, c, lax.rem(z + NZ - d, NZ)]
            remote(slot, send_z.at[d - 1], recv_z.at[d - 1], z_peer(d)).wait_recv()
        for d in range(1, NY):
            send(remote(columns.at[y, x, c], send_y.at[d - 1], recv_y.at[d - 1], y_peer(d)))

    def router_x():
        for d in range(1, NY):
            slot = columns.at[lax.rem(y + NY - d, NY), x, c]
            remote(slot, send_y.at[d - 1], recv_y.at[d - 1], y_peer(d)).wait_recv()
        for d in range(1, NX):
            send(remote(columns.at[:, x, c], send_x.at[d - 1], recv_x.at[d - 1], x_peer(d)))

    def router_c():
        for d in range(1, NX):
            slot = columns.at[:, lax.rem(x + NX - d, NX), c]
            remote(slot, send_x.at[d - 1], recv_x.at[d - 1], x_peer(d)).wait_recv()
        send(remote(columns.at[:, :, c], send_c, recv_c, c_peer()))

    def router_out():
        slot = columns.at[:, :, NC - 1 - c]
        remote(slot, send_c, recv_c, c_peer()).wait_recv()
        for j in range(NZ * 2):
            part = columns[:, :, :, j // 2, j % 2, :].reshape(NY * NX * NC, LANES)
            router_ref[:, j * LANES : (j + 1) * LANES] = part.astype(jnp.bfloat16)

    extras = {(0, 6): router_y, (1, 1): router_x, (1, 5): router_c, (2, 2): router_out}
    for step in range(FULL_STEPS):
        last = step + 1 == FULL_STEPS
        for k in range(CHUNKS):
            arrive_up(step, k)
            if not last or k < HALF:
                send(chunk_up(step + 1, k))
            arrive_dn(step, k)
            if not last or k >= HALF:
                send(chunk_dn(step + 1, k))
            if (step, k) in extras:
                extras[step, k]()
    for k in range(HALF):
        arrive_up(FULL_STEPS, k)
        arrive_dn(FULL_STEPS, k + HALF)
    for copy in sent:
        copy.wait_send()


def place_kernel(blocks_ref, router_ref, down_out, router_out, sem, router_sem):
    copies = []
    for b in range(NZ):
        for k in range(CHUNKS):
            dst = down_out.at[pl.ds(b * CUT, CUT), pl.ds(k * LANES, LANES)]
            copies.append(pltpu.make_async_copy(blocks_ref.at[b, k], dst, sem.at[b, k]))
    copies.append(pltpu.make_async_copy(router_ref, router_out, router_sem))
    for copy in copies:
        copy.start()
    for copy in copies:
        copy.wait()


def on_device(train_down, router_weight, router_gain):
    anywhere = pl.BlockSpec(memory_space=pltpu.HBM)
    vmem = pl.BlockSpec(memory_space=pltpu.VMEM)
    owners = NY * NX * NC
    dma = pltpu.SemaphoreType.DMA
    blocks, router = pl.pallas_call(
        gather_kernel,
        name="gather",
        out_shape=(
            jax.ShapeDtypeStruct((NZ, CHUNKS, CUT, LANES), jnp.bfloat16),
            jax.ShapeDtypeStruct((owners, NZ * CUT), jnp.bfloat16),
        ),
        in_specs=[anywhere] * 3,
        out_specs=(vmem, vmem),
        scratch_shapes=[
            pltpu.VMEM((EXPERT, CUT), jnp.float32),
            pltpu.VMEM((2, LANES), jnp.float32),
            pltpu.VMEM((2, LANES), jnp.float32),
            pltpu.VMEM((NY, NX, NC, NZ, 2, LANES), jnp.float32),
            dma((CHUNKS,)),
            dma((2,)),
            dma((EVENTS,)), dma((EVENTS,)), dma((EVENTS,)), dma((EVENTS,)),
            dma((NZ - 1,)), dma((NZ - 1,)),
            dma((NY - 1,)), dma((NY - 1,)),
            dma((NX - 1,)), dma((NX - 1,)),
            dma, dma,
        ],
        compiler_params=pltpu.CompilerParams(
            collective_id=0, has_side_effects=True, vmem_limit_bytes=16 << 20
        ),
    )(
        *(pltpu.with_memory_space_constraint(array, pltpu.HBM) for array in (
            train_down.reshape(EXPERT, CUT),
            router_weight.reshape(2, LANES),
            router_gain.reshape(2, LANES),
        )),
    )
    ready, serve = pl.pallas_call(
        place_kernel,
        name="place",
        out_shape=(
            jax.ShapeDtypeStruct((NZ * CUT, EXPERT), jnp.bfloat16),
            jax.ShapeDtypeStruct((owners, NZ * CUT), jnp.bfloat16),
        ),
        in_specs=[vmem, vmem],
        out_specs=(anywhere, anywhere),
        scratch_shapes=[dma((NZ, CHUNKS)), dma],
        compiler_params=pltpu.CompilerParams(vmem_limit_bytes=16 << 20),
    )(blocks, router)
    return ready[None], serve.T


def solution(mesh):
    in_specs = (P("owner", None, "rows"), P("rows", "owner"), P("rows"))
    out_specs = (P("owner", None, None), P())
    return jax.shard_map(
        on_device, mesh=mesh, in_specs=in_specs, out_specs=out_specs, check_vma=False
    )
```

time: 85.9 us -> 60.6 us (0.71)
  Pallas kernels: 0 us -> 59.8 us
  blocking collectives: 46.8 us -> 0 us
  between operations: 14.1 us -> 0.64 us
  waiting for transfers between devices: 12.9 us -> 0 us
  local copies, waits for them, and re-layouts: 8.91 us -> 0 us
  other arithmetic: 2.89 us -> 0 us
    pallas_call x0 -> x2, Pallas kernels: none -> 59.8 us  [the longest x1 57.2 us: on_device(): pl.pallas_call(gather_kernel, name='gather', out_shape=(jax.ShapeDtypeStr...]
    all_to_all x1 -> x0, blocking collectives: 27.4 us -> none  [from_everyone(): return lax.all_to_all(copies, axis, split_axis=0, concat_axis=0, tiled=True)]
    all_gather x1 -> x0, blocking collectives: 19.4 us -> none  [on_device(): row_router = lax.all_gather(part_router, 'rows', axis=0, tiled=True)]
    all_gather x1 -> x0, waiting for transfers between devices: 12.9 us -> none  [on_device(): ready_down = lax.all_gather(narrow_down, 'rows', axis=2, tiled=True)]
    unnamed x6 -> x0, local copies, waits for them, and re-layouts: 8.05 us -> none
    unnamed x1 -> x0, other arithmetic: 2.15 us -> none
  transfers between devices with their start and end apart: 1 -> 0, of which waited for: 1 -> 0; matrix products, arithmetic and copies ran while one was open for 6% -> 0% of each run, Pallas kernels for 0% -> 0%
where the time goes in v1:
time: 60.6 us; the launch traced here: 60.4 us
  Pallas kernels  59.8 us (99%)
  between operations  0.64 us (1%)
    pallas_call x1, Pallas kernels, on_device(): pl.pallas_call(gather_kernel, name='gather', out_shape=(jax.ShapeDtypeStr...  57.2 us
    pallas_call x1, Pallas kernels, on_device(): pl.pallas_call(place_kernel, name='place', out_shape=(jax.ShapeDtypeStruc...  2.63 us

profile of v1, /device:TPU:1, one launch (start us, length us, event | category | flops | bytes accessed | tf_op | source)
XLA Modules:
  0.0 60.4 jit_solution(447825585754319560)
XLA Ops:
  0.6 57.2 %gather.1 = (bf16[8,8,256,128]{3,2,1,0:T(8,128)(2,1)S(1)}, bf16[64,2048]{1,0:T(8,128)(2,1)S(1)}) custom-call(f32[1024,256]{1,0:T(8,128)} %bitcast.5, f32[2,128]{1,0:T(2,128)} %bitcast.6, f32[2,128]{1,0:T(2,128)} %bitcast.7), custom_call_target="tpu_custom_call" | custom-call | tf_op jit(solution)/shard_map/gather/pallas_call | solution.py:184
  57.8 2.6 %place.1 = (bf16[2048,1024]{1,0:T(8,128)(2,1)}, bf16[64,2048]{1,0:T(8,128)(2,1)}) custom-call(bf16[8,8,256,128]{3,2,1,0:T(8,128)(2,1)S(1)} %get-tuple-element.6.blocks_ref, bf16[64,2048]{1,0:T(8,128)(2,1)S(1)} %get-tuple-element.7.router_ref), custom_call_target="tpu_custom_call" | custom-call | tf_op jit(solution)/shard_map/place/pallas_call | solution.py:216

commit v2 on v1

--- a/solution.py
+++ b/solution.py
@@ -13,9 +13,17 @@
 CUT = 256
 LANES = 128
 CHUNKS = EXPERT // LANES
-HALF = CHUNKS // 2
 FULL_STEPS = NZ // 2 - 1
-EVENTS = FULL_STEPS * CHUNKS + HALF
+EVENTS = (FULL_STEPS + 1) * CHUNKS
+ROUNDS = 3
+SHARE = (2, 3, 4, 4, 4, 4, 4, 4)
+
+
+def share_of(z):
+    share = jnp.int32(SHARE[NZ - 1])
+    for place in range(NZ - 1):
+        share = jnp.where(z == place, jnp.int32(SHARE[place]), share)
+    return share
 
 
 def gather_kernel(
@@ -23,6 +31,7 @@
     blocks_ref, router_ref,
     down, weight, gain, columns,
     in_sem, small_sem,
+    round_sem,
     send_up, recv_up, send_dn, recv_dn,
     send_z, recv_z, send_y, recv_y, send_x, recv_x, send_c, recv_c,
 ):
@@ -60,10 +69,16 @@
         loads[k].start()
 
     barrier = pltpu.get_barrier_semaphore()
-    peers = [z_peer(d) for d in range(1, NZ)] + [y_peer(d) for d in range(1, NY)]
-    peers += [x_peer(d) for d in range(1, NX)] + [c_peer()]
-    for peer in peers:
-        pl.semaphore_signal(barrier, inc=1, device_id=peer, device_id_type=MESH)
+    near = [z_peer(1), z_peer(NZ - 1), y_peer(1), y_peer(NY - 1), x_peer(1), x_peer(NX - 1)]
+
+    def greet(sem, peers):
+        for peer in peers:
+            pl.semaphore_signal(sem, inc=1, device_id=peer, device_id_type=MESH)
+
+    greet(barrier, [*near, c_peer()])
+    share = share_of(z)
+    share_above = share_of(lax.rem(z + 1, NZ))
+    share_below = share_of(lax.rem(z + NZ - 1, NZ))
 
     def turn(k):
         loads[k].wait()
@@ -83,7 +98,7 @@
 
     def chunk_dn(step, k):
         slot = blocks_ref.at[lax.rem(z + step, NZ), k]
-        i = step * CHUNKS + (k if step < FULL_STEPS else k - HALF)
+        i = step * CHUNKS + k
         return remote(slot, send_dn.at[i], recv_dn.at[i], z_peer(NZ - 1))
 
     def arrive_up(step, k):
@@ -93,29 +108,38 @@
 
     def arrive_dn(step, k):
         slot = blocks_ref.at[lax.rem(z + step + 1, NZ), k]
-        i = step * CHUNKS + (k if step < FULL_STEPS else k - HALF)
+        i = step * CHUNKS + k
         remote(slot, send_dn.at[i], recv_dn.at[i], z_peer(NZ - 1)).wait_recv()
 
     sent = []
 
-    def send(copy):
-        copy.start()
-        sent.append(copy)
+    def send(copy, when=None):
+        if when is None:
+            copy.start()
+        else:
+            pl.when(when)(copy.start)
+        sent.append((copy, when))
 
     turn(0)
     load_weight.wait()
     load_gain.wait()
     columns[y, x, c, z] = weight[...] * gain[...]
     turn(1)
-    pl.semaphore_wait(barrier, len(peers))
-
-    for d in range(1, NZ):
-        send(remote(columns.at[y, x, c, z], send_z.at[d - 1], recv_z.at[d - 1], z_peer(d)))
+    pl.semaphore_wait(barrier, len(near) + 1)
+
     for k in range(CHUNKS):
         if k >= 1 and k + 1 < CHUNKS:
             turn(k + 1)
         send(chunk_up(0, k))
         send(chunk_dn(0, k))
+        if k == 0:
+            greet(round_sem.at[0], near)
+    for r in range(ROUNDS):
+        pl.semaphore_wait(round_sem.at[r], len(near))
+        if r + 1 < ROUNDS:
+            greet(round_sem.at[r + 1], near)
+    for d in range(1, NZ):
+        send(remote(columns.at[y, x, c, z], send_z.at[d - 1], recv_z.at[d - 1], z_peer(d)))
 
     def router_y():
         for d in range(1, NZ):
@@ -144,23 +168,24 @@
             part = columns[:, :, :, j // 2, j % 2, :].reshape(NY * NX * NC, LANES)
             router_ref[:, j * LANES : (j + 1) * LANES] = part.astype(jnp.bfloat16)
 
-    extras = {(0, 6): router_y, (1, 1): router_x, (1, 5): router_c, (2, 2): router_out}
+    extras = {9: router_y, 14: router_x, 17: router_c, 20: router_out}
     for step in range(FULL_STEPS):
         last = step + 1 == FULL_STEPS
         for k in range(CHUNKS):
             arrive_up(step, k)
-            if not last or k < HALF:
-                send(chunk_up(step + 1, k))
+            send(chunk_up(step + 1, k), k < share_above if last else None)
             arrive_dn(step, k)
-            if not last or k >= HALF:
-                send(chunk_dn(step + 1, k))
-            if (step, k) in extras:
-                extras[step, k]()
-    for k in range(HALF):
-        arrive_up(FULL_STEPS, k)
-        arrive_dn(FULL_STEPS, k + HALF)
-    for copy in sent:
-        copy.wait_send()
+            send(chunk_dn(step + 1, k), k >= share_below if last else None)
+            if step * CHUNKS + k in extras:
+                extras[step * CHUNKS + k]()
+    for k in range(CHUNKS):
+        pl.when(k < share)(functools.partial(arrive_up, FULL_STEPS, k))
+        pl.when(k >= share)(functools.partial(arrive_dn, FULL_STEPS, k))
+    for copy, when in sent:
+        if when is None:
+            copy.wait_send()
+        else:
+            pl.when(when)(copy.wait_send)
 
 
 def place_kernel(blocks_ref, router_ref, down_out, router_out, sem, router_sem):
@@ -197,6 +222,7 @@
             pltpu.VMEM((NY, NX, NC, NZ, 2, LANES), jnp.float32),
             dma((CHUNKS,)),
             dma((2,)),
+            pltpu.SemaphoreType.REGULAR((ROUNDS,)),
             dma((EVENTS,)), dma((EVENTS,)), dma((EVENTS,)), dma((EVENTS,)),
             dma((NZ - 1,)), dma((NZ - 1,)),
             dma((NY - 1,)), dma((NY - 1,)),

time: 60.6 us -> 55.6 us (0.917)
  Pallas kernels: 59.8 us -> 54.7 us
    pallas_call x1, Pallas kernels: 57.2 us -> 52 us  [on_device(): pl.pallas_call(gather_kernel, name='gather', out_shape=(jax.ShapeDtypeStr...]
where the time goes in v2:
time: 55.6 us; the launch traced here: 55.3 us
  Pallas kernels  54.7 us (98%)
  between operations  0.64 us (1%)
    pallas_call x1, Pallas kernels, on_device(): pl.pallas_call(gather_kernel, name='gather', out_shape=(jax.ShapeDtypeStr...  52 us
    pallas_call x1, Pallas kernels, on_device(): pl.pallas_call(place_kernel, name='place', out_shape=(jax.ShapeDtypeStruc...  2.63 us

profile of v2, /device:TPU:1, one launch (start us, length us, event | category | flops | bytes accessed | tf_op | source)
XLA Modules:
  0.0 55.3 jit_solution(236357807196732564)
XLA Ops:
  0.6 52.0 %gather.1 = (bf16[8,8,256,128]{3,2,1,0:T(8,128)(2,1)S(1)}, bf16[64,2048]{1,0:T(8,128)(2,1)S(1)}) custom-call(f32[1024,256]{1,0:T(8,128)} %bitcast.5, f32[2,128]{1,0:T(2,128)} %bitcast.6, f32[2,128]{1,0:T(2,128)} %bitcast.7), custom_call_target="tpu_custom_call" | custom-call | tf_op jit(solution)/shard_map/gather/pallas_call | solution.py:209
  52.7 2.6 %place.1 = (bf16[2048,1024]{1,0:T(8,128)(2,1)}, bf16[64,2048]{1,0:T(8,128)(2,1)}) custom-call(bf16[8,8,256,128]{3,2,1,0:T(8,128)(2,1)S(1)} %get-tuple-element.6.blocks_ref, bf16[64,2048]{1,0:T(8,128)(2,1)S(1)} %get-tuple-element.7.router_ref), custom_call_target="tpu_custom_call" | custom-call | tf_op jit(solution)/shard_map/place/pallas_call | solution.py:242

commit v3 on v0

v3 whole, which is shorter than its diff:
```python
import functools

import jax
import jax.numpy as jnp
from jax import lax
from jax.experimental import pallas as pl
from jax.experimental.pallas import tpu as pltpu
from jax.sharding import PartitionSpec as P

MESH = pl.DeviceIdType.MESH
NY, NX, NC, NZ = 8, 4, 2, 8
EXPERT = 1024
CUT = 256
LANES = 128
PIECES = EXPERT // LANES
GROUP = 1
CHUNKS = PIECES // GROUP
STEPS = NZ // 2 - 1
ROUNDS = 3
SHARE = (2, 4, 4, 4, 4, 4, 4, 6)
STAGES = (12, 19, 21, 23)
MEET, MEET_ROUNDS = 4, (6, 8, 10)
UP, DOWN, NORTH, SOUTH, EAST, WEST, TWIN = range(7)
BACK = (DOWN, UP, SOUTH, NORTH, WEST, EAST, TWIN)


def share_of(z):
    share = jnp.int32(SHARE[NZ - 1])
    for place in range(NZ - 1):
        share = jnp.where(z == place, jnp.int32(SHARE[place]), share)
    return share


def gather_kernel(
    down_ref, weight_ref, gain_ref,
    blocks_ref, router_ref,
    down, factors, columns,
    load_sem, small_sem, met_sem, along_sem, across_sem,
    send_sem, last_sem, recv_sem, recv_last,
    send_part, recv_part,
):
    owner = lax.axis_index("owner")
    z = lax.axis_index("rows")
    c = lax.rem(owner, NC)
    x = lax.rem(owner // NC, NX)
    y = owner // (NC * NX)

    edges = (1, 2, PIECES)
    loads = []
    for n, (low, high) in enumerate(zip((0, *edges), edges)):
        part = pl.ds(low * LANES, (high - low) * LANES)
        loads.append(pltpu.make_async_copy(down_ref.at[part], down.at[part], load_sem.at[n]))
    small = [
        pltpu.make_async_copy(weight_ref, factors.at[0], small_sem),
        pltpu.make_async_copy(gain_ref, factors.at[1], small_sem),
    ]
    loads[0].start()
    loads[1].start()
    small[0].start()
    small[1].start()
    loads[2].start()

    def device(yy, xx, cc, zz):
        return {"owner": (yy * NX + xx) * NC + cc, "rows": zz}

    def z_peer(d):
        return device(y, x, c, lax.rem(z + d, NZ))

    def y_peer(d):
        return device(lax.rem(y + d, NY), x, c, z)

    def x_peer(d):
        return device(y, lax.rem(x + d, NX), c, z)

    c_peer = device(y, x, NC - 1 - c, z)
    near = [z_peer(1), z_peer(NZ - 1), y_peer(1), y_peer(NY - 1), x_peer(1), x_peer(NX - 1)]
    near.append(c_peer)
    later = [
        z != NZ - 1, z == 0,
        y < NY // 2, jnp.logical_or(y > NY // 2, y == 0),
        x != NX - 1, x == 0,
        c == NC - 1,
    ]

    def tell(sem, peer):
        pl.semaphore_signal(sem, inc=1, device_id=peer, device_id_type=MESH)

    barrier = pltpu.get_barrier_semaphore()
    for peer, after in zip(near, later):
        pl.when(after)(functools.partial(tell, barrier, peer))
    earlier = sum(jnp.where(after, 0, 1) for after in later)

    def meet(i):
        pl.when(later[i])(lambda: pl.semaphore_wait(met_sem.at[i], 1))

    def met_at(i):
        return met_sem.at[min(BACK[i], NORTH)]

    share = share_of(z)
    share_above = share_of(lax.rem(z + 1, NZ))
    share_below = share_of(lax.rem(z + NZ - 1, NZ))

    def turn(k):
        piece = down[k * LANES : (k + 1) * LANES, :]
        blocks_ref[z, k] = jnp.transpose(piece).astype(jnp.bfloat16)

    def remote(ref, send, recv, peer):
        return pltpu.make_async_remote_copy(
            src_ref=ref, dst_ref=ref, send_sem=send, recv_sem=recv,
            device_id=peer, device_id_type=MESH,
        )

    def chunk_of(block, k):
        return blocks_ref.at[lax.rem(block, NZ), pl.ds(k * GROUP, GROUP)]

    def copy_up(step, k, block):
        return remote(chunk_of(block, k), send_sem, recv_sem.at[step * CHUNKS + k], near[UP])

    def copy_dn(step, k, block):
        return remote(chunk_of(block, k), send_sem, recv_sem.at[step * CHUNKS + k], near[DOWN])

    def end_up(k):
        slot = blocks_ref.at[lax.rem(z + NZ - STEPS, NZ), k]
        return remote(slot, last_sem.at[UP], recv_last, near[UP])

    def end_dn(k):
        slot = blocks_ref.at[lax.rem(z + STEPS, NZ), k]
        return remote(slot, last_sem.at[DOWN], recv_last, near[DOWN])

    def own_up(k):
        copy_up(0, k, z).start()

    def own_dn(k):
        copy_dn(0, k, z).start()

    pl.when(earlier > 0)(lambda: pl.semaphore_wait(barrier, earlier))
    for i, peer in enumerate(near):
        pl.when(jnp.logical_not(later[i]))(functools.partial(tell, met_at(i), peer))
    loads[0].wait()
    turn(0)
    loads[1].wait()
    turn(1)
    top, bottom = z == NZ - 1, z == 0
    ready = 2
    for k in range(CHUNKS):
        while ready < min((k + 1) * GROUP + 1, PIECES):
            if ready == 2:
                loads[2].wait()
            turn(ready)
            ready += 1
        pl.when(jnp.logical_not(bottom))(functools.partial(own_dn, k))
        pl.when(top)(functools.partial(own_up, k))
    meet(UP)
    for k in range(CHUNKS):
        pl.when(jnp.logical_not(top))(functools.partial(own_up, k))
    pltpu.make_async_copy(factors, factors, small_sem).wait()
    columns[y, x, c, z] = factors[0] * factors[1]
    meet(DOWN)
    for k in range(CHUNKS):
        pl.when(bottom)(functools.partial(own_dn, k))
    for r in range(ROUNDS):
        for peer in near[:NORTH]:
            tell(along_sem.at[r], peer)
        pl.semaphore_wait(along_sem.at[r], 2)

    def meet_across():
        count = sum(jnp.where(after, 1, 0) for after in later[NORTH:])
        pl.when(count > 0)(lambda: pl.semaphore_wait(met_sem.at[NORTH], count))
        for peer in near[NORTH:TWIN]:
            tell(across_sem.at[0], peer)

    def meet_round(r):
        pl.semaphore_wait(across_sem.at[r], 4)
        if r + 1 < ROUNDS:
            for peer in near[NORTH:TWIN]:
                tell(across_sem.at[r + 1], peer)

    def part(i, ref, peer):
        return remote(ref, send_part.at[i], recv_part.at[i], peer)

    own = columns.at[y, x, c, z]
    for d in range(1, NZ):
        part(0, own, z_peer(d)).start()

    def router_y():
        part(0, columns.at[y, x, c, pl.ds(0, NZ - 1)], z_peer(1)).wait_recv()
        for d in range(1, NY):
            part(1, columns.at[y, x, c], y_peer(d)).start()

    def router_x():
        part(1, columns.at[pl.ds(0, NY - 1), x, c], y_peer(1)).wait_recv()
        for d in range(1, NX):
            part(2, columns.at[:, x, c], x_peer(d)).start()

    def router_c():
        part(2, columns.at[:, pl.ds(0, NX - 1), c], x_peer(1)).wait_recv()
        part(3, columns.at[:, :, c], c_peer).start()

    def router_out():
        part(3, columns.at[:, :, NC - 1 - c], c_peer).wait_recv()
        for j in range(NZ * 2):
            piece = columns[:, :, :, j // 2, j % 2, :].reshape(NY * NX * NC, LANES)
            router_ref[:, j * LANES : (j + 1) * LANES] = piece.astype(jnp.bfloat16)

    stages = dict(zip(STAGES, (router_y, router_x, router_c, router_out)))
    stages[MEET] = meet_across
    stages.update((at, functools.partial(meet_round, r)) for r, at in enumerate(MEET_ROUNDS))
    for step in range(STEPS):
        for k in range(CHUNKS):
            both = blocks_ref.at[0, pl.ds(0, 2 * GROUP)]
            remote(both, send_sem, recv_sem.at[step * CHUNKS + k], near[UP]).wait_recv()
            if step + 1 < STEPS:
                copy_up(step + 1, k, z + NZ - step - 1).start()
                copy_dn(step + 1, k, z + step + 1).start()
            else:
                for n in range(k * GROUP, (k + 1) * GROUP):
                    if n < max(SHARE):
                        pl.when(n < share_above)(lambda n=n: end_up(n).start())
                    if n >= min(SHARE):
                        pl.when(n >= share_below)(lambda n=n: end_dn(n).start())
            for n in range(GROUP):
                if (step * CHUNKS + k) * GROUP + n in stages:
                    stages[(step * CHUNKS + k) * GROUP + n]()

    sent = blocks_ref.at[pl.ds(0, 2 * STEPS)]
    remote(sent, send_sem, recv_sem.at[0], near[UP]).wait_send()
    for n in sorted(set(SHARE)):
        up, dn = blocks_ref.at[0, pl.ds(0, n)], blocks_ref.at[0, pl.ds(n, PIECES - n)]
        pl.when(share_above == n)(remote(up, last_sem.at[UP], recv_last, near[UP]).wait_send)
        pl.when(share_below == n)(remote(dn, last_sem.at[DOWN], recv_last, near[DOWN]).wait_send)
    part(0, columns.at[y, x, c, pl.ds(0, NZ - 1)], z_peer(1)).wait_send()
    part(1, columns.at[pl.ds(0, NY - 1), x, c], y_peer(1)).wait_send()
    part(2, columns.at[:, pl.ds(0, NX - 1), c], x_peer(1)).wait_send()
    part(3, columns.at[:, :, c], c_peer).wait_send()
    far = blocks_ref.at[lax.rem(z + NZ // 2, NZ)]
    remote(far, last_sem.at[UP], recv_last, near[UP]).wait_recv()


def place_kernel(blocks_ref, router_ref, down_out, router_out, sem, router_sem):
    for b in range(NZ):
        for k in range(PIECES):
            dst = down_out.at[pl.ds(b * CUT, CUT), pl.ds(k * LANES, LANES)]
            pltpu.make_async_copy(blocks_ref.at[b, k], dst, sem).start()
    router = pltpu.make_async_copy(router_ref, router_out, router_sem)
    router.start()
    pltpu.make_async_copy(blocks_ref, blocks_ref, sem).wait()
    router.wait()


def on_device(train_down, router_weight, router_gain):
    hbm = pl.BlockSpec(memory_space=pltpu.HBM)
    vmem = pl.BlockSpec(memory_space=pltpu.VMEM)
    owners = NY * NX * NC
    dma, plain = pltpu.SemaphoreType.DMA, pltpu.SemaphoreType.REGULAR
    blocks, router = pl.pallas_call(
        gather_kernel,
        name="gather",
        out_shape=(
            jax.ShapeDtypeStruct((NZ, PIECES, CUT, LANES), jnp.bfloat16),
            jax.ShapeDtypeStruct((owners, NZ * CUT), jnp.bfloat16),
        ),
        in_specs=[hbm] * 3,
        out_specs=(vmem, vmem),
        scratch_shapes=[
            pltpu.VMEM((EXPERT, CUT), jnp.float32),
            pltpu.VMEM((2, 2, LANES), jnp.float32),
            pltpu.VMEM((NY, NX, NC, NZ, 2, LANES), jnp.float32),
            dma((3,)), dma, plain((NORTH + 1,)), plain((ROUNDS,)), plain((ROUNDS,)),
            dma, dma((2,)), dma((STEPS * CHUNKS,)), dma,
            dma((4,)), dma((4,)),
        ],
        compiler_params=pltpu.CompilerParams(
            collective_id=0, has_side_effects=True, vmem_limit_bytes=16 << 20
        ),
    )(
        *(pltpu.with_memory_space_constraint(array, pltpu.HBM) for array in (
            train_down.reshape(EXPERT, CUT),
            router_weight.reshape(2, LANES),
            router_gain.reshape(2, LANES),
        )),
    )
    ready, serve = pl.pallas_call(
        place_kernel,
        name="place",
        out_shape=(
            jax.ShapeDtypeStruct((NZ * CUT, EXPERT), jnp.bfloat16),
            jax.ShapeDtypeStruct((owners, NZ * CUT), jnp.bfloat16),
        ),
        in_specs=[vmem, vmem],
        out_specs=(hbm, hbm),
        scratch_shapes=[dma, dma],
        compiler_params=pltpu.CompilerParams(vmem_limit_bytes=16 << 20),
    )(blocks, router)
    return ready[None], serve.T


def solution(mesh):
    in_specs = (P("owner", None, "rows"), P("rows", "owner"), P("rows"))
    out_specs = (P("owner", None, None), P())
    return jax.shard_map(
        on_device, mesh=mesh, in_specs=in_specs, out_specs=out_specs, check_vma=False
    )
```

time: 85.9 us -> 53 us (0.62)
  Pallas kernels: 0 us -> 52.2 us
  blocking collectives: 46.8 us -> 0 us
  between operations: 14.1 us -> 0.64 us
  waiting for transfers between devices: 12.9 us -> 0 us
  local copies, waits for them, and re-layouts: 8.91 us -> 0 us
  other arithmetic: 2.89 us -> 0 us
    pallas_call x0 -> x2, Pallas kernels: none -> 52.2 us  [the longest x1 50.1 us: on_device(): pl.pallas_call(gather_kernel, name='gather', out_shape=(jax.ShapeDtypeStr...]
    all_to_all x1 -> x0, blocking collectives: 27.4 us -> none  [from_everyone(): return lax.all_to_all(copies, axis, split_axis=0, concat_axis=0, tiled=True)]
    all_gather x1 -> x0, blocking collectives: 19.4 us -> none  [on_device(): row_router = lax.all_gather(part_router, 'rows', axis=0, tiled=True)]
    all_gather x1 -> x0, waiting for transfers between devices: 12.9 us -> none  [on_device(): ready_down = lax.all_gather(narrow_down, 'rows', axis=2, tiled=True)]
    unnamed x6 -> x0, local copies, waits for them, and re-layouts: 8.05 us -> none
    unnamed x1 -> x0, other arithmetic: 2.15 us -> none
  transfers between devices with their start and end apart: 1 -> 0, of which waited for: 1 -> 0; matrix products, arithmetic and copies ran while one was open for 6% -> 0% of each run, Pallas kernels for 0% -> 0%
where the time goes in v3:
time: 53 us; the launch traced here: 52.8 us
  Pallas kernels  52.2 us (98%)
  between operations  0.64 us (1%)
    pallas_call x1, Pallas kernels, on_device(): pl.pallas_call(gather_kernel, name='gather', out_shape=(jax.ShapeDtypeStr...  50.1 us
    pallas_call x1, Pallas kernels, on_device(): pl.pallas_call(place_kernel, name='place', out_shape=(jax.ShapeDtypeStruc...  2.07 us

profile of v3, /device:TPU:1, one launch (start us, length us, event | category | flops | bytes accessed | tf_op | source)
XLA Modules:
  0.0 52.8 jit_solution(4372707106760220658)
XLA Ops:
  0.6 50.1 %gather.1 = (bf16[8,8,256,128]{3,2,1,0:T(8,128)(2,1)S(1)}, bf16[64,2048]{1,0:T(8,128)(2,1)S(1)}) custom-call(f32[1024,256]{1,0:T(8,128)} %bitcast.5, f32[2,128]{1,0:T(2,128)} %bitcast.6, f32[2,128]{1,0:T(2,128)} %bitcast.7), custom_call_target="tpu_custom_call" | custom-call | tf_op jit(solution)/shard_map/gather/pallas_call | solution.py:255
  50.7 2.1 %place.1 = (bf16[2048,1024]{1,0:T(8,128)(2,1)}, bf16[64,2048]{1,0:T(8,128)(2,1)}) custom-call(bf16[8,8,256,128]{3,2,1,0:T(8,128)(2,1)S(1)} %get-tuple-element.6.blocks_ref, bf16[64,2048]{1,0:T(8,128)(2,1)S(1)} %get-tuple-element.7.router_ref), custom_call_target="tpu_custom_call" | custom-call | tf_op jit(solution)/shard_map/place/pallas_call | solution.py:282

commit v4 on v3

--- a/solution.py
+++ b/solution.py
@@ -18,8 +18,8 @@
 STEPS = NZ // 2 - 1
 ROUNDS = 3
 SHARE = (2, 4, 4, 4, 4, 4, 4, 6)
-STAGES = (12, 19, 21, 23)
-MEET, MEET_ROUNDS = 4, (6, 8, 10)
+STAGES = (10, 15, 18, 20)
+MEET, MEET_ROUNDS = 3, (5, 7, 9)
 UP, DOWN, NORTH, SOUTH, EAST, WEST, TWIN = range(7)
 BACK = (DOWN, UP, SOUTH, NORTH, WEST, EAST, TWIN)
 
@@ -81,6 +81,12 @@
         x != NX - 1, x == 0,
         c == NC - 1,
     ]
+    place = ((c * NZ + z) * NY + y) * NX + x
+    first = place == 0
+    for i, at in ((DOWN, NY * NX), (NORTH, (NY - 1) * NX), (SOUTH, NX), (EAST, NX - 1), (WEST, 1)):
+        later[i] = jnp.logical_or(later[i], place == at)
+    for i in (UP, NORTH, SOUTH, EAST, WEST):
+        later[i] = jnp.logical_and(later[i], jnp.logical_not(first))
 
     def tell(sem, peer):
         pl.semaphore_signal(sem, inc=1, device_id=peer, device_id_type=MESH)
@@ -140,7 +146,6 @@
     turn(0)
     loads[1].wait()
     turn(1)
-    top, bottom = z == NZ - 1, z == 0
     ready = 2
     for k in range(CHUNKS):
         while ready < min((k + 1) * GROUP + 1, PIECES):
@@ -148,16 +153,16 @@
                 loads[2].wait()
             turn(ready)
             ready += 1
-        pl.when(jnp.logical_not(bottom))(functools.partial(own_dn, k))
-        pl.when(top)(functools.partial(own_up, k))
+        pl.when(jnp.logical_not(later[DOWN]))(functools.partial(own_dn, k))
+        pl.when(jnp.logical_not(later[UP]))(functools.partial(own_up, k))
     meet(UP)
     for k in range(CHUNKS):
-        pl.when(jnp.logical_not(top))(functools.partial(own_up, k))
+        pl.when(later[UP])(functools.partial(own_up, k))
     pltpu.make_async_copy(factors, factors, small_sem).wait()
     columns[y, x, c, z] = factors[0] * factors[1]
     meet(DOWN)
     for k in range(CHUNKS):
-        pl.when(bottom)(functools.partial(own_dn, k))
+        pl.when(later[DOWN])(functools.partial(own_dn, k))
     for r in range(ROUNDS):
         for peer in near[:NORTH]:
             tell(along_sem.at[r], peer)

time: 53 us -> 51.8 us (0.977)
  Pallas kernels: 52.2 us -> 51 us
    pallas_call x1, Pallas kernels: 50.1 us -> 48.9 us  [on_device(): pl.pallas_call(gather_kernel, name='gather', out_shape=(jax.ShapeDtypeStr...]
where the time goes in v4:
time: 51.8 us; the launch traced here: 51.6 us
  Pallas kernels  51 us (98%)
  between operations  0.64 us (1%)
    pallas_call x1, Pallas kernels, on_device(): pl.pallas_call(gather_kernel, name='gather', out_shape=(jax.ShapeDtypeStr...  48.9 us
    pallas_call x1, Pallas kernels, on_device(): pl.pallas_call(place_kernel, name='place', out_shape=(jax.ShapeDtypeStruc...  2.07 us

profile of v4, /device:TPU:1, one launch (start us, length us, event | category | flops | bytes accessed | tf_op | source)
XLA Modules:
  0.0 51.6 jit_solution(16285715669474200229)
XLA Ops:
  0.6 48.9 %gather.1 = (bf16[8,8,256,128]{3,2,1,0:T(8,128)(2,1)S(1)}, bf16[64,2048]{1,0:T(8,128)(2,1)S(1)}) custom-call(f32[1024,256]{1,0:T(8,128)} %bitcast.5, f32[2,128]{1,0:T(2,128)} %bitcast.6, f32[2,128]{1,0:T(2,128)} %bitcast.7), custom_call_target="tpu_custom_call" | custom-call | tf_op jit(solution)/shard_map/gather/pallas_call | solution.py:260
  49.6 2.1 %place.1 = (bf16[2048,1024]{1,0:T(8,128)(2,1)}, bf16[64,2048]{1,0:T(8,128)(2,1)}) custom-call(bf16[8,8,256,128]{3,2,1,0:T(8,128)(2,1)S(1)} %get-tuple-element.6.blocks_ref, bf16[64,2048]{1,0:T(8,128)(2,1)S(1)} %get-tuple-element.7.router_ref), custom_call_target="tpu_custom_call" | custom-call | tf_op jit(solution)/shard_map/place/pallas_call | solution.py:287

commit v5 on v4

--- a/solution.py
+++ b/solution.py
@@ -13,31 +13,34 @@
 CUT = 256
 LANES = 128
 PIECES = EXPERT // LANES
-GROUP = 1
+GROUP = 2
 CHUNKS = PIECES // GROUP
 STEPS = NZ // 2 - 1
 ROUNDS = 3
-SHARE = (2, 4, 4, 4, 4, 4, 4, 6)
+SHARE = ((1, 4, 4, 4, 4, 4, 4, 6), (2, 4, 4, 4, 4, 4, 4, 6))
+CORNER_SHARE = 1
 STAGES = (10, 15, 18, 20)
 MEET, MEET_ROUNDS = 3, (5, 7, 9)
 UP, DOWN, NORTH, SOUTH, EAST, WEST, TWIN = range(7)
 BACK = (DOWN, UP, SOUTH, NORTH, WEST, EAST, TWIN)
 
 
-def share_of(z):
-    share = jnp.int32(SHARE[NZ - 1])
-    for place in range(NZ - 1):
-        share = jnp.where(z == place, jnp.int32(SHARE[place]), share)
-    return share
+def share_of(corner, c, z):
+    share = jnp.int32(0)
+    for core in range(NC):
+        for place in range(NZ):
+            share = jnp.where(jnp.logical_and(c == core, z == place), jnp.int32(SHARE[core][place]), share)
+    at_start = jnp.logical_and(corner, jnp.logical_and(c == NC - 1, z == 0))
+    return jnp.where(at_start, jnp.int32(CORNER_SHARE), share)
 
 
 def gather_kernel(
     down_ref, weight_ref, gain_ref,
     blocks_ref, router_ref,
     down, factors, columns,
-    load_sem, small_sem, met_sem, along_sem, across_sem,
+    load_sem, small_sem, met_sem, across_sem,
     send_sem, last_sem, recv_sem, recv_last,
-    send_part, recv_part,
+    part_sem,
 ):
     owner = lax.axis_index("owner")
     z = lax.axis_index("rows")
@@ -45,7 +48,7 @@
     x = lax.rem(owner // NC, NX)
     y = owner // (NC * NX)
 
-    edges = (1, 2, PIECES)
+    edges = (2, PIECES)
     loads = []
     for n, (low, high) in enumerate(zip((0, *edges), edges)):
         part = pl.ds(low * LANES, (high - low) * LANES)
@@ -55,10 +58,9 @@
         pltpu.make_async_copy(gain_ref, factors.at[1], small_sem),
     ]
     loads[0].start()
-    loads[1].start()
     small[0].start()
     small[1].start()
-    loads[2].start()
+    loads[1].start()
 
     def device(yy, xx, cc, zz):
         return {"owner": (yy * NX + xx) * NC + cc, "rows": zz}
@@ -102,9 +104,14 @@
     def met_at(i):
         return met_sem.at[min(BACK[i], NORTH)]
 
-    share = share_of(z)
-    share_above = share_of(lax.rem(z + 1, NZ))
-    share_below = share_of(lax.rem(z + NZ - 1, NZ))
+    corner = jnp.logical_and(y == 0, x == 0)
+    share_above = share_of(corner, c, lax.rem(z + 1, NZ))
+    share_below = share_of(corner, c, lax.rem(z + NZ - 1, NZ))
+
+    def comes_up(share, n):
+        few = share <= PIECES // 2
+        return jnp.logical_or(jnp.logical_and(few, n < share), jnp.logical_and(jnp.logical_not(few), n >= PIECES - share))
+
 
     def turn(k):
         piece = down[k * LANES : (k + 1) * LANES, :]
@@ -133,40 +140,38 @@
         slot = blocks_ref.at[lax.rem(z + STEPS, NZ), k]
         return remote(slot, last_sem.at[DOWN], recv_last, near[DOWN])
 
-    def own_up(k):
-        copy_up(0, k, z).start()
-
-    def own_dn(k):
-        copy_dn(0, k, z).start()
+    def own_up(n):
+        remote(blocks_ref.at[z, n], send_sem, recv_sem.at[n // GROUP], near[UP]).start()
+
+    def own_dn(n):
+        remote(blocks_ref.at[z, n], send_sem, recv_sem.at[n // GROUP], near[DOWN]).start()
 
     pl.when(earlier > 0)(lambda: pl.semaphore_wait(barrier, earlier))
     for i, peer in enumerate(near):
         pl.when(jnp.logical_not(later[i]))(functools.partial(tell, met_at(i), peer))
     loads[0].wait()
     turn(0)
-    loads[1].wait()
     turn(1)
-    ready = 2
-    for k in range(CHUNKS):
-        while ready < min((k + 1) * GROUP + 1, PIECES):
-            if ready == 2:
-                loads[2].wait()
-            turn(ready)
-            ready += 1
-        pl.when(jnp.logical_not(later[DOWN]))(functools.partial(own_dn, k))
-        pl.when(jnp.logical_not(later[UP]))(functools.partial(own_up, k))
+    for n in range(PIECES):
+        if n == 1:
+            loads[1].wait()
+        if 1 <= n < PIECES - 1:
+            turn(n + 1)
+        pl.when(jnp.logical_not(later[DOWN]))(functools.partial(own_dn, n))
+        pl.when(jnp.logical_not(later[UP]))(functools.partial(own_up, n))
     meet(UP)
-    for k in range(CHUNKS):
-        pl.when(later[UP])(functools.partial(own_up, k))
+    for n in range(PIECES):
+        pl.when(later[UP])(functools.partial(own_up, n))
     pltpu.make_async_copy(factors, factors, small_sem).wait()
     columns[y, x, c, z] = factors[0] * factors[1]
     meet(DOWN)
-    for k in range(CHUNKS):
-        pl.when(later[DOWN])(functools.partial(own_dn, k))
-    for r in range(ROUNDS):
-        for peer in near[:NORTH]:
-            tell(along_sem.at[r], peer)
-        pl.semaphore_wait(along_sem.at[r], 2)
+    for n in range(PIECES):
+        pl.when(later[DOWN])(functools.partial(own_dn, n))
+    for _ in range(ROUNDS):
+        for i in (UP, DOWN):
+            tell(met_at(i), near[i])
+        for i in (UP, DOWN):
+            pl.semaphore_wait(met_sem.at[i], 1)
 
     def meet_across():
         count = sum(jnp.where(after, 1, 0) for after in later[NORTH:])
@@ -181,33 +186,36 @@
                 tell(across_sem.at[r + 1], peer)
 
     def part(i, ref, peer):
-        return remote(ref, send_part.at[i], recv_part.at[i], peer)
+        return remote(ref, part_sem.at[i], part_sem.at[i], peer)
 
     own = columns.at[y, x, c, z]
     for d in range(1, NZ):
         part(0, own, z_peer(d)).start()
 
     def router_y():
-        part(0, columns.at[y, x, c, pl.ds(0, NZ - 1)], z_peer(1)).wait_recv()
+        part(0, columns.at[y, x, :, pl.ds(0, NZ - 1)], z_peer(1)).wait_recv()
         for d in range(1, NY):
             part(1, columns.at[y, x, c], y_peer(d)).start()
 
     def router_x():
-        part(1, columns.at[pl.ds(0, NY - 1), x, c], y_peer(1)).wait_recv()
+        part(1, columns.at[pl.ds(0, NY - 1), x], y_peer(1)).wait_recv()
         for d in range(1, NX):
             part(2, columns.at[:, x, c], x_peer(d)).start()
 
     def router_c():
-        part(2, columns.at[:, pl.ds(0, NX - 1), c], x_peer(1)).wait_recv()
+        part(2, columns.at[:, pl.ds(0, NX - 1)], x_peer(1)).wait_recv()
         part(3, columns.at[:, :, c], c_peer).start()
 
     def router_out():
-        part(3, columns.at[:, :, NC - 1 - c], c_peer).wait_recv()
+        part(3, columns, c_peer).wait_recv()
         for j in range(NZ * 2):
             piece = columns[:, :, :, j // 2, j % 2, :].reshape(NY * NX * NC, LANES)
             router_ref[:, j * LANES : (j + 1) * LANES] = piece.astype(jnp.bfloat16)
 
-    stages = dict(zip(STAGES, (router_y, router_x, router_c, router_out)))
+    feeder = z == 1
+    stages = dict(zip(STAGES, (router_y, router_x)))
+    for at, stage in zip(STAGES[2:], (router_c, router_out)):
+        stages[at] = functools.partial(pl.when(jnp.logical_not(feeder)), stage)
     stages[MEET] = meet_across
     stages.update((at, functools.partial(meet_round, r)) for r, at in enumerate(MEET_ROUNDS))
     for step in range(STEPS):
@@ -219,24 +227,26 @@
                 copy_dn(step + 1, k, z + step + 1).start()
             else:
                 for n in range(k * GROUP, (k + 1) * GROUP):
-                    if n < max(SHARE):
-                        pl.when(n < share_above)(lambda n=n: end_up(n).start())
-                    if n >= min(SHARE):
-                        pl.when(n >= share_below)(lambda n=n: end_dn(n).start())
+                    pl.when(comes_up(share_above, n))(lambda n=n: end_up(n).start())
+                    pl.when(jnp.logical_not(comes_up(share_below, n)))(lambda n=n: end_dn(n).start())
             for n in range(GROUP):
                 if (step * CHUNKS + k) * GROUP + n in stages:
                     stages[(step * CHUNKS + k) * GROUP + n]()
 
+    @pl.when(feeder)
+    def _():
+        router_c()
+        router_out()
+
     sent = blocks_ref.at[pl.ds(0, 2 * STEPS)]
     remote(sent, send_sem, recv_sem.at[0], near[UP]).wait_send()
-    for n in sorted(set(SHARE)):
-        up, dn = blocks_ref.at[0, pl.ds(0, n)], blocks_ref.at[0, pl.ds(n, PIECES - n)]
-        pl.when(share_above == n)(remote(up, last_sem.at[UP], recv_last, near[UP]).wait_send)
-        pl.when(share_below == n)(remote(dn, last_sem.at[DOWN], recv_last, near[DOWN]).wait_send)
-    part(0, columns.at[y, x, c, pl.ds(0, NZ - 1)], z_peer(1)).wait_send()
-    part(1, columns.at[pl.ds(0, NY - 1), x, c], y_peer(1)).wait_send()
-    part(2, columns.at[:, pl.ds(0, NX - 1), c], x_peer(1)).wait_send()
-    part(3, columns.at[:, :, c], c_peer).wait_send()
+    for n in sorted({*SHARE[0], *SHARE[1], CORNER_SHARE}):
+        if n > 0:
+            up = blocks_ref.at[0, pl.ds(0, n)]
+            pl.when(share_above == n)(remote(up, last_sem.at[UP], recv_last, near[UP]).wait_send)
+        if n < PIECES:
+            dn = blocks_ref.at[0, pl.ds(0, PIECES - n)]
+            pl.when(share_below == n)(remote(dn, last_sem.at[DOWN], recv_last, near[DOWN]).wait_send)
     far = blocks_ref.at[lax.rem(z + NZ // 2, NZ)]
     remote(far, last_sem.at[UP], recv_last, near[UP]).wait_recv()
 
@@ -270,9 +280,9 @@
             pltpu.VMEM((EXPERT, CUT), jnp.float32),
             pltpu.VMEM((2, 2, LANES), jnp.float32),
             pltpu.VMEM((NY, NX, NC, NZ, 2, LANES), jnp.float32),
-            dma((3,)), dma, plain((NORTH + 1,)), plain((ROUNDS,)), plain((ROUNDS,)),
+            dma((2,)), dma, plain((NORTH + 1,)), plain((ROUNDS,)),
             dma, dma((2,)), dma((STEPS * CHUNKS,)), dma,
-            dma((4,)), dma((4,)),
+            dma((4,)),
         ],
         compiler_params=pltpu.CompilerParams(
             collective_id=0, has_side_effects=True, vmem_limit_bytes=16 << 20

time: 51.8 us -> 51.6 us (level)
  no operation moved by 1% of the time
where the time goes in v5:
time: 51.6 us; the launch traced here: 51.4 us
  Pallas kernels  50.8 us (98%)
  between operations  0.64 us (1%)
    pallas_call x1, Pallas kernels, on_device(): pl.pallas_call(gather_kernel, name='gather', out_shape=(jax.ShapeDtypeStr...  48.7 us
    pallas_call x1, Pallas kernels, on_device(): pl.pallas_call(place_kernel, name='place', out_shape=(jax.ShapeDtypeStruc...  2.07 us

profile of v5, /device:TPU:1, one launch (start us, length us, event | category | flops | bytes accessed | tf_op | source)
XLA Modules:
  0.0 51.4 jit_solution(14520302202818236812)
XLA Ops:
  0.6 48.7 %gather.1 = (bf16[8,8,256,128]{3,2,1,0:T(8,128)(2,1)S(1)}, bf16[64,2048]{1,0:T(8,128)(2,1)S(1)}) custom-call(f32[1024,256]{1,0:T(8,128)} %bitcast.5, f32[2,128]{1,0:T(2,128)} %bitcast.6, f32[2,128]{1,0:T(2,128)} %bitcast.7), custom_call_target="tpu_custom_call" | custom-call | tf_op jit(solution)/shard_map/gather/pallas_call | solution.py:270
  49.4 2.1 %place.1 = (bf16[2048,1024]{1,0:T(8,128)(2,1)}, bf16[64,2048]{1,0:T(8,128)(2,1)}) custom-call(bf16[8,8,256,128]{3,2,1,0:T(8,128)(2,1)S(1)} %get-tuple-element.6.blocks_ref, bf16[64,2048]{1,0:T(8,128)(2,1)S(1)} %get-tuple-element.7.router_ref), custom_call_target="tpu_custom_call" | custom-call | tf_op jit(solution)/shard_map/place/pallas_call | solution.py:297

commit v6 on v5

--- a/solution.py
+++ b/solution.py
@@ -21,6 +21,7 @@
 CORNER_SHARE = 1
 STAGES = (10, 15, 18, 20)
 MEET, MEET_ROUNDS = 3, (5, 7, 9)
+AHEAD = 2
 UP, DOWN, NORTH, SOUTH, EAST, WEST, TWIN = range(7)
 BACK = (DOWN, UP, SOUTH, NORTH, WEST, EAST, TWIN)
 
@@ -167,6 +168,20 @@
     meet(DOWN)
     for n in range(PIECES):
         pl.when(later[DOWN])(functools.partial(own_dn, n))
+    def forward(step, k):
+        both = blocks_ref.at[0, pl.ds(0, 2 * GROUP)]
+        remote(both, send_sem, recv_sem.at[step * CHUNKS + k], near[UP]).wait_recv()
+        if step + 1 < STEPS:
+            copy_up(step + 1, k, z + NZ - step - 1).start()
+            copy_dn(step + 1, k, z + step + 1).start()
+        else:
+            for n in range(k * GROUP, (k + 1) * GROUP):
+                pl.when(comes_up(share_above, n))(lambda n=n: end_up(n).start())
+                pl.when(jnp.logical_not(comes_up(share_below, n)))(lambda n=n: end_dn(n).start())
+
+    feeder = z == 1
+    for k in range(AHEAD):
+        pl.when(feeder)(functools.partial(forward, 0, k))
     for _ in range(ROUNDS):
         for i in (UP, DOWN):
             tell(met_at(i), near[i])
@@ -212,7 +227,6 @@
             piece = columns[:, :, :, j // 2, j % 2, :].reshape(NY * NX * NC, LANES)
             router_ref[:, j * LANES : (j + 1) * LANES] = piece.astype(jnp.bfloat16)
 
-    feeder = z == 1
     stages = dict(zip(STAGES, (router_y, router_x)))
     for at, stage in zip(STAGES[2:], (router_c, router_out)):
         stages[at] = functools.partial(pl.when(jnp.logical_not(feeder)), stage)
@@ -220,15 +234,10 @@
     stages.update((at, functools.partial(meet_round, r)) for r, at in enumerate(MEET_ROUNDS))
     for step in range(STEPS):
         for k in range(CHUNKS):
-            both = blocks_ref.at[0, pl.ds(0, 2 * GROUP)]
-            remote(both, send_sem, recv_sem.at[step * CHUNKS + k], near[UP]).wait_recv()
-            if step + 1 < STEPS:
-                copy_up(step + 1, k, z + NZ - step - 1).start()
-                copy_dn(step + 1, k, z + step + 1).start()
+            if step * CHUNKS + k < AHEAD:
+                pl.when(jnp.logical_not(feeder))(functools.partial(forward, step, k))
             else:
-                for n in range(k * GROUP, (k + 1) * GROUP):
-                    pl.when(comes_up(share_above, n))(lambda n=n: end_up(n).start())
-                    pl.when(jnp.logical_not(comes_up(share_below, n)))(lambda n=n: end_dn(n).start())
+                forward(step, k)
             for n in range(GROUP):
                 if (step * CHUNKS + k) * GROUP + n in stages:
                     stages[(step * CHUNKS + k) * GROUP + n]()

time: 51.6 us -> 50.9 us (0.986); the launches traced: 51.4 us -> 50 us
  Pallas kernels: 50.8 us -> 49.3 us
    pallas_call x1, Pallas kernels: 48.7 us -> 47.3 us  [on_device(): pl.pallas_call(gather_kernel, name='gather', out_shape=(jax.ShapeDtypeStr...]
where the time goes in v6:
time: 50.9 us; the launch traced here: 50 us
  Pallas kernels  49.3 us (97%)
  between operations  0.64 us (1%)
    pallas_call x1, Pallas kernels, on_device(): pl.pallas_call(gather_kernel, name='gather', out_shape=(jax.ShapeDtypeStr...  47.3 us
    pallas_call x1, Pallas kernels, on_device(): pl.pallas_call(place_kernel, name='place', out_shape=(jax.ShapeDtypeStruc...  2.07 us

profile of v6, /device:TPU:1, one launch (start us, length us, event | category | flops | bytes accessed | tf_op | source)
XLA Modules:
  0.0 50.0 jit_solution(4111773067318782020)
XLA Ops:
  0.6 47.3 %gather.1 = (bf16[8,8,256,128]{3,2,1,0:T(8,128)(2,1)S(1)}, bf16[64,2048]{1,0:T(8,128)(2,1)S(1)}) custom-call(f32[1024,256]{1,0:T(8,128)} %bitcast.5, f32[2,128]{1,0:T(2,128)} %bitcast.6, f32[2,128]{1,0:T(2,128)} %bitcast.7), custom_call_target="tpu_custom_call" | custom-call | tf_op jit(solution)/shard_map/gather/pallas_call | solution.py:279
  47.9 2.1 %place.1 = (bf16[2048,1024]{1,0:T(8,128)(2,1)}, bf16[64,2048]{1,0:T(8,128)(2,1)}) custom-call(bf16[8,8,256,128]{3,2,1,0:T(8,128)(2,1)S(1)} %get-tuple-element.6.blocks_ref, bf16[64,2048]{1,0:T(8,128)(2,1)S(1)} %get-tuple-element.7.router_ref), custom_call_target="tpu_custom_call" | custom-call | tf_op jit(solution)/shard_map/place/pallas_call | solution.py:306

commit v7 on v6

--- a/solution.py
+++ b/solution.py
@@ -19,7 +19,7 @@
 ROUNDS = 3
 SHARE = ((1, 4, 4, 4, 4, 4, 4, 6), (2, 4, 4, 4, 4, 4, 4, 6))
 CORNER_SHARE = 1
-STAGES = (10, 15, 18, 20)
+STAGES = (8, 10, 15, 18, 20)
 MEET, MEET_ROUNDS = 3, (5, 7, 9)
 AHEAD = 2
 UP, DOWN, NORTH, SOUTH, EAST, WEST, TWIN = range(7)
@@ -38,7 +38,7 @@
 def gather_kernel(
     down_ref, weight_ref, gain_ref,
     blocks_ref, router_ref,
-    down, factors, columns,
+    down, factors, rounded, columns,
     load_sem, small_sem, met_sem, across_sem,
     send_sem, last_sem, recv_sem, recv_last,
     part_sem,
@@ -164,7 +164,7 @@
     for n in range(PIECES):
         pl.when(later[UP])(functools.partial(own_up, n))
     pltpu.make_async_copy(factors, factors, small_sem).wait()
-    columns[y, x, c, z] = factors[0] * factors[1]
+    rounded[z] = (factors[0] * factors[1]).astype(jnp.bfloat16)
     meet(DOWN)
     for n in range(PIECES):
         pl.when(later[DOWN])(functools.partial(own_dn, n))
@@ -203,12 +203,15 @@
     def part(i, ref, peer):
         return remote(ref, part_sem.at[i], part_sem.at[i], peer)
 
-    own = columns.at[y, x, c, z]
+    own = rounded.at[z]
     for d in range(1, NZ):
         part(0, own, z_peer(d)).start()
 
+    def router_z():
+        part(0, columns.at[y, x, c, pl.ds(0, NZ - 1)], z_peer(1)).wait_recv()
+        columns[y, x, c] = rounded[...].astype(jnp.float32)
+
     def router_y():
-        part(0, columns.at[y, x, :, pl.ds(0, NZ - 1)], z_peer(1)).wait_recv()
         for d in range(1, NY):
             part(1, columns.at[y, x, c], y_peer(d)).start()
 
@@ -227,8 +230,8 @@
             piece = columns[:, :, :, j // 2, j % 2, :].reshape(NY * NX * NC, LANES)
             router_ref[:, j * LANES : (j + 1) * LANES] = piece.astype(jnp.bfloat16)
 
-    stages = dict(zip(STAGES, (router_y, router_x)))
-    for at, stage in zip(STAGES[2:], (router_c, router_out)):
+    stages = dict(zip(STAGES, (router_z, router_y, router_x)))
+    for at, stage in zip(STAGES[3:], (router_c, router_out)):
         stages[at] = functools.partial(pl.when(jnp.logical_not(feeder)), stage)
     stages[MEET] = meet_across
     stages.update((at, functools.partial(meet_round, r)) for r, at in enumerate(MEET_ROUNDS))
@@ -288,6 +291,7 @@
         scratch_shapes=[
             pltpu.VMEM((EXPERT, CUT), jnp.float32),
             pltpu.VMEM((2, 2, LANES), jnp.float32),
+            pltpu.VMEM((NZ, 2, LANES), jnp.bfloat16),
             pltpu.VMEM((NY, NX, NC, NZ, 2, LANES), jnp.float32),
             dma((2,)), dma, plain((NORTH + 1,)), plain((ROUNDS,)),
             dma, dma((2,)), dma((STEPS * CHUNKS,)), dma,

time: 50.9 us -> 50.8 us (level)
  no operation moved by 1% of the time
where the time goes in v7:
time: 50.8 us; the launch traced here: 49.9 us
  Pallas kernels  49.2 us (97%)
  between operations  0.64 us (1%)
    pallas_call x1, Pallas kernels, on_device(): pl.pallas_call(gather_kernel, name='gather', out_shape=(jax.ShapeDtypeStr...  47.2 us
    pallas_call x1, Pallas kernels, on_device(): pl.pallas_call(place_kernel, name='place', out_shape=(jax.ShapeDtypeStruc...  2.07 us

profile of v7, /device:TPU:1, one launch (start us, length us, event | category | flops | bytes accessed | tf_op | source)
XLA Modules:
  0.0 49.9 jit_solution(3119287431862863371)
XLA Ops:
  0.6 47.2 %gather.1 = (bf16[8,8,256,128]{3,2,1,0:T(8,128)(2,1)S(1)}, bf16[64,2048]{1,0:T(8,128)(2,1)S(1)}) custom-call(f32[1024,256]{1,0:T(8,128)} %bitcast.5, f32[2,128]{1,0:T(2,128)} %bitcast.6, f32[2,128]{1,0:T(2,128)} %bitcast.7), custom_call_target="tpu_custom_call" | custom-call | tf_op jit(solution)/shard_map/gather/pallas_call | solution.py:282
  47.8 2.1 %place.1 = (bf16[2048,1024]{1,0:T(8,128)(2,1)}, bf16[64,2048]{1,0:T(8,128)(2,1)}) custom-call(bf16[8,8,256,128]{3,2,1,0:T(8,128)(2,1)S(1)} %get-tuple-element.6.blocks_ref, bf16[64,2048]{1,0:T(8,128)(2,1)S(1)} %get-tuple-element.7.router_ref), custom_call_target="tpu_custom_call" | custom-call | tf_op jit(solution)/shard_map/place/pallas_call | solution.py:310

commit v8 on v7

--- a/solution.py
+++ b/solution.py
@@ -154,9 +154,10 @@
     turn(0)
     turn(1)
     for n in range(PIECES):
-        if n == 1:
+        if n == 2:
             loads[1].wait()
-        if 1 <= n < PIECES - 1:
+            turn(2)
+        if 2 <= n < PIECES - 1:
             turn(n + 1)
         pl.when(jnp.logical_not(later[DOWN]))(functools.partial(own_dn, n))
         pl.when(jnp.logical_not(later[UP]))(functools.partial(own_up, n))

time: 50.8 us -> 50.8 us (level)
  no operation moved by 1% of the time
where the time goes in v8:
time: 50.8 us; the launch traced here: 49.9 us
  Pallas kernels  49.2 us (97%)
  between operations  0.64 us (1%)
    pallas_call x1, Pallas kernels, on_device(): pl.pallas_call(gather_kernel, name='gather', out_shape=(jax.ShapeDtypeStr...  47.2 us
    pallas_call x1, Pallas kernels, on_device(): pl.pallas_call(place_kernel, name='place', out_shape=(jax.ShapeDtypeStruc...  2.07 us

profile of v8, /device:TPU:1, one launch (start us, length us, event | category | flops | bytes accessed | tf_op | source)
XLA Modules:
  0.0 49.9 jit_solution(13218619732605071841)
XLA Ops:
  0.6 47.2 %gather.1 = (bf16[8,8,256,128]{3,2,1,0:T(8,128)(2,1)S(1)}, bf16[64,2048]{1,0:T(8,128)(2,1)S(1)}) custom-call(f32[1024,256]{1,0:T(8,128)} %bitcast.5, f32[2,128]{1,0:T(2,128)} %bitcast.6, f32[2,128]{1,0:T(2,128)} %bitcast.7), custom_call_target="tpu_custom_call" | custom-call | tf_op jit(solution)/shard_map/gather/pallas_call | solution.py:283
  47.8 2.1 %place.1 = (bf16[2048,1024]{1,0:T(8,128)(2,1)}, bf16[64,2048]{1,0:T(8,128)(2,1)}) custom-call(bf16[8,8,256,128]{3,2,1,0:T(8,128)(2,1)S(1)} %get-tuple-element.6.blocks_ref, bf16[64,2048]{1,0:T(8,128)(2,1)S(1)} %get-tuple-element.7.router_ref), custom_call_target="tpu_custom_call" | custom-call | tf_op jit(solution)/shard_map/place/pallas_call | solution.py:311
